TPU v7x, 32 devices: a whole 2x2x4 slice. The times are simulated.
32 devices in a mesh: dp: 8 (over y, x, core), tensor: 4 (over z).
Axes of the slice: x: 2, y: 2, z: 4, core: 2. Of those that a mesh axis runs over, the one named last changes fastest.
Arguments:
- layer_input: float32 [16, 512, 2048], P('dp', 'tensor'), may hold values from -6 to 6
- segments: int32 [16, 512], P('dp'), may hold values from 0 to 7, never falling along the last dimension, each value on 1 to 256 neighbouring positions
- gain_attn: bfloat16 [2048], P('dp'), may hold values from 0.5 to 1.5
- w_qkv: bfloat16 [2048, 4, 640], P('dp', 'tensor'), as said below
- w_out_t: bfloat16 [2048, 2048], P('dp', 'tensor'), may hold values from -0.75 to 0.75
- gain_mlp: bfloat16 [2048], P('dp'), may hold values from 0.5 to 1.5
- w_gate_up: bfloat16 [2048, 2, 5632], P('dp', None, 'tensor'), may hold values from -0.125 to 0.125
- w_down_t: bfloat16 [2048, 5632], P('dp', 'tensor'), may hold values from -0.078125 to 0.078125
- cotangent: float32 [16, 512, 2048], P('dp', 'tensor'), may hold values from -6 to 6
Outputs:
- output: float32 [16, 512, 2048], P('dp', 'tensor')
- input_grad: float32 [16, 512, 2048], P('dp', 'tensor')
- gain_attn_grad: float32 [2048], P('dp')
- qkv_grad: float32 [2048, 4, 640], P('dp', 'tensor')
- out_grad: float32 [2048, 2048], P('dp', 'tensor')
- gain_mlp_grad: float32 [2048], P('dp')
- gate_up_grad: float32 [2048, 2, 5632], P('dp', None, 'tensor')
- down_grad: float32 [2048, 5632], P('dp', 'tensor')
Inputs may be any that keep to these rules, and one draw needn't show every extreme that they name: `w_qkv`: for each key-value group the columns hold the queries of its 8 heads, then its key, then its value.
All inputs are finite; a program needn't handle non-finite values.
Results may differ from a plain program's by a relative error of at most 0.013.
Values may be sent and summed in bfloat16 or wider, within the bound.
A program may use at most 256 MiB of HBM per device.

v0:
```python
import math
import jax
import jax.numpy as jnp
from jax import lax
from jax.sharding import PartitionSpec as P

H = 32
KV = 4
HD = 64
NORM_EPS = 1e-05


def rope_tables(segment_row, head_size):
    row_count = segment_row.shape[0]
    earlier = jnp.sum((segment_row[None, :] < segment_row[:, None]).astype(jnp.int32), axis=1)
    position = (jnp.arange(row_count, dtype=jnp.int32) - earlier).astype(jnp.float32)
    half_size = head_size // 2
    frequency = jnp.exp(
        jnp.arange(half_size, dtype=jnp.float32) * (-2.0 * math.log(10000.0) / head_size)
    )
    angles = position[:, None] * frequency[None, :]
    return (jnp.cos(angles), jnp.sin(angles))


def expand_table(angle_table, rank_count):
    return angle_table.reshape(
        (angle_table.shape[0],) + (1,) * (rank_count - 2) + (angle_table.shape[1],)
    )


def rotate(values, cosine, sine_tab):
    half_size = values.shape[-1] // 2
    cosine = expand_table(cosine, values.ndim)
    sine_tab = expand_table(sine_tab, values.ndim)
    first_half = values[..., :half_size]
    second_half = values[..., half_size:]
    return jnp.concatenate(
        [
            first_half * cosine - second_half * sine_tab,
            second_half * cosine + first_half * sine_tab,
        ],
        axis=-1,
    )


def unrotate(values, cosine, sine_tab):
    half_size = values.shape[-1] // 2
    cosine = expand_table(cosine, values.ndim)
    sine_tab = expand_table(sine_tab, values.ndim)
    first_half = values[..., :half_size]
    second_half = values[..., half_size:]
    return jnp.concatenate(
        [
            first_half * cosine + second_half * sine_tab,
            second_half * cosine - first_half * sine_tab,
        ],
        axis=-1,
    )


def allowed_pairs(segment_row):
    row_count = segment_row.shape[0]
    position = jnp.arange(row_count, dtype=jnp.int32)
    return (segment_row[:, None] == segment_row[None, :]) & (position[None, :] <= position[:, None])


def norm_forward(row_block, gain_row):
    inv_rms = lax.rsqrt(jnp.mean(row_block * row_block, axis=-1, keepdims=True) + NORM_EPS)
    return ((row_block * inv_rms * gain_row.astype(jnp.float32)).astype(jnp.bfloat16), inv_rms)


def norm_backward(row_block, inv_rms, gain_row, upstream):
    weighted = upstream * gain_row.astype(jnp.float32)
    back_term = inv_rms * weighted - row_block * (inv_rms * inv_rms * inv_rms) * jnp.mean(
        weighted * row_block, axis=-1, keepdims=True
    )
    return (back_term, jnp.sum(upstream * row_block * inv_rms, axis=0))


def split_heads(qkv_rows, head_group, head_size):
    row_count, groups = (qkv_rows.shape[0], qkv_rows.shape[1])
    query = qkv_rows[:, :, : head_group * head_size].reshape(
        row_count, groups, head_group, head_size
    )
    key_part = qkv_rows[:, :, head_group * head_size : (head_group + 1) * head_size]
    value_part = qkv_rows[:, :, (head_group + 1) * head_size :]
    return (query, key_part, value_part)


def score_block(query, key_part, allowed, head_size):
    scores = jnp.einsum("igne,jge->gnij", query, key_part, preferred_element_type=jnp.float32) * (
        1.0 / math.sqrt(head_size)
    )
    return jnp.where(allowed[None, None], scores, jnp.float32(-1e30))


def attend_forward(qkv_rows, segment_row, head_group, head_size):
    cosine, sine_tab = rope_tables(segment_row, head_size)
    query, key_part, value_part = split_heads(qkv_rows, head_group, head_size)
    query = rotate(query, cosine, sine_tab).astype(jnp.bfloat16)
    key_part = rotate(key_part, cosine, sine_tab).astype(jnp.bfloat16)
    value_part = value_part.astype(jnp.bfloat16)
    allowed = allowed_pairs(segment_row)
    scores = score_block(query, key_part, allowed, head_size)
    row_max = jnp.max(scores, axis=-1, keepdims=True)
    log_total = row_max + jnp.log(jnp.sum(jnp.exp(scores - row_max), axis=-1, keepdims=True))
    weights = jnp.exp(scores - log_total).astype(jnp.bfloat16)
    mixed = jnp.einsum("gnij,jge->igne", weights, value_part, preferred_element_type=jnp.float32)
    mixed = mixed.astype(jnp.bfloat16).reshape(qkv_rows.shape[0], -1)
    return (mixed, (query, key_part, value_part, log_total, cosine, sine_tab, allowed))


def attend_backward(grad_out, saved, head_size):
    query, key_part, value_part, log_total, cosine, sine_tab, allowed = saved
    row_count, groups, head_group = (query.shape[0], query.shape[1], query.shape[2])
    scores = score_block(query, key_part, allowed, head_size)
    weights = jnp.exp(scores - log_total)
    grad_heads = grad_out.reshape(row_count, groups, head_group, head_size)
    grad_value = jnp.einsum(
        "gnij,igne->jge",
        weights.astype(jnp.bfloat16),
        grad_heads,
        preferred_element_type=jnp.float32,
    )
    grad_weights = jnp.einsum(
        "igne,jge->gnij", grad_heads, value_part, preferred_element_type=jnp.float32
    )
    grad_scores = (
        weights
        * (grad_weights - jnp.sum(weights * grad_weights, axis=-1, keepdims=True))
        * (1.0 / math.sqrt(head_size))
    )
    grad_scores = grad_scores.astype(jnp.bfloat16)
    grad_query = jnp.einsum(
        "gnij,jge->igne", grad_scores, key_part, preferred_element_type=jnp.float32
    )
    grad_key = jnp.einsum("gnij,igne->jge", grad_scores, query, preferred_element_type=jnp.float32)
    grad_query = unrotate(grad_query, cosine, sine_tab).reshape(
        row_count, groups, head_group * head_size
    )
    grad_key = unrotate(grad_key, cosine, sine_tab)
    return jnp.concatenate([grad_query, grad_key, grad_value], axis=2).astype(jnp.bfloat16)


def outer_product(left_rows, right_rows):
    return lax.dot_general(
        left_rows, right_rows, (((0,), (0,)), ((), ())), preferred_element_type=jnp.float32
    )


def right_product(left_rows, right_matrix):
    return lax.dot_general(
        left_rows, right_matrix, (((1,), (1,)), ((), ())), preferred_element_type=jnp.float32
    )


def spread_forward(row_block):
    return lax.all_gather(row_block, "tensor", axis=0, tiled=True)


def spread_backward(row_block):
    return lax.all_gather(row_block, "tensor", axis=0, tiled=True)


def branch_sum(term_fn, local_rows):
    return lax.psum_scatter(
        term_fn(jnp.int32(0), lax.axis_size("tensor") * local_rows),
        "tensor",
        scatter_dimension=0,
        tiled=True,
    )


def input_sum(term_fn, local_rows):
    return lax.psum_scatter(
        term_fn(jnp.int32(0), lax.axis_size("tensor") * local_rows),
        "tensor",
        scatter_dimension=0,
        tiled=True,
    )


def add_terms(left_terms, right_terms):
    if left_terms is None:
        return right_terms
    return tuple((left_term + right_term for left_term, right_term in zip(left_terms, right_terms)))


def body(
    layer_input, segments, gain_attn, w_qkv, w_out_t, gain_mlp, w_gate_up, w_down_t, cotangent
):
    head_group = H // KV
    weight_shard = (gain_attn, w_qkv, w_out_t, gain_mlp, w_gate_up, w_down_t)
    local_rows = layer_input.shape[1]
    outputs = []
    input_grads = []
    grad_total = None
    owned_grads = None
    for number in range(layer_input.shape[0]):
        gathered_weights = (
            lax.all_gather(weight_shard[0], "dp", axis=0, tiled=True),
            lax.all_gather(weight_shard[1], "dp", axis=0, tiled=True),
            lax.all_gather(weight_shard[2], "dp", axis=0, tiled=True),
            lax.all_gather(weight_shard[3], "dp", axis=0, tiled=True),
            lax.all_gather(weight_shard[4], "dp", axis=0, tiled=True),
            lax.all_gather(weight_shard[5], "dp", axis=0, tiled=True),
        )
        g_attn, qkv_w, out_w, g_mlp, gu_w, down_w = gathered_weights
        model_width = qkv_w.shape[0]
        groups = qkv_w.shape[1]
        hidden_width = gu_w.shape[2]
        segment_row = segments[number]
        rows_in = layer_input[number]
        normed_attn, scale_attn = norm_forward(rows_in, g_attn)
        gathered_attn = spread_forward(normed_attn)
        row_count = gathered_attn.shape[0]
        qkv_rows = jnp.dot(
            gathered_attn, qkv_w.reshape(model_width, -1), preferred_element_type=jnp.float32
        ).reshape(row_count, groups, -1)
        mixed, saved = attend_forward(qkv_rows, segment_row, head_group, HD)

        def attn_term(row_start, row_span):
            return right_product(mixed, out_w)

        residual = rows_in + branch_sum(attn_term, local_rows)
        normed_mlp, scale_mlp = norm_forward(residual, g_mlp)
        gathered_mlp = spread_forward(normed_mlp)
        gate_up = jnp.dot(
            gathered_mlp, gu_w.reshape(model_width, -1), preferred_element_type=jnp.float32
        ).reshape(row_count, 2, hidden_width)
        gate_part = gate_up[:, 0]
        up_part = gate_up[:, 1]
        sigmoid_gate = jax.nn.sigmoid(gate_part)
        active = gate_part * sigmoid_gate
        hidden = (active * up_part).astype(jnp.bfloat16)

        def mlp_term(row_start, row_span):
            return right_product(hidden, down_w)

        outputs.append(residual + branch_sum(mlp_term, local_rows))
        back_weights = (
            lax.all_gather(weight_shard[0], "dp", axis=0, tiled=True),
            lax.all_gather(weight_shard[1], "dp", axis=0, tiled=True),
            lax.all_gather(weight_shard[2], "dp", axis=0, tiled=True),
            lax.all_gather(weight_shard[3], "dp", axis=0, tiled=True),
            lax.all_gather(weight_shard[4], "dp", axis=0, tiled=True),
            lax.all_gather(weight_shard[5], "dp", axis=0, tiled=True),
        )
        g_attn, qkv_w, out_w, g_mlp, gu_w, down_w = back_weights
        grad_in = cotangent[number]
        grad_rows = spread_backward(grad_in.astype(jnp.bfloat16))
        grad_down = outer_product(grad_rows, hidden)
        grad_hidden = jnp.dot(grad_rows, down_w, preferred_element_type=jnp.float32)
        grad_gu = jnp.stack(
            [
                grad_hidden * up_part * sigmoid_gate * (1.0 + gate_part * (1.0 - sigmoid_gate)),
                grad_hidden * active,
            ],
            axis=1,
        ).astype(jnp.bfloat16)
        flat_gu = grad_gu.reshape(row_count, -1)
        grad_gu_w = outer_product(gathered_mlp, flat_gu).reshape(model_width, 2, hidden_width)
        gu_flat = gu_w.reshape(model_width, -1)

        def mlp_back(row_start, row_span):
            return right_product(flat_gu, gu_flat)

        grad_normed_mlp = input_sum(mlp_back, local_rows)
        back_mlp, grad_g_mlp = norm_backward(residual, scale_mlp, g_mlp, grad_normed_mlp)
        grad_resid = grad_in + back_mlp
        resid_rows = spread_backward(grad_resid.astype(jnp.bfloat16))
        grad_out_w = outer_product(resid_rows, mixed)
        grad_mixed = jnp.dot(resid_rows, out_w, preferred_element_type=jnp.float32).astype(
            jnp.bfloat16
        )
        grad_qkv = attend_backward(grad_mixed, saved, HD)
        flat_qkv = grad_qkv.reshape(row_count, -1)
        grad_qkv_w = outer_product(gathered_attn, flat_qkv).reshape(qkv_w.shape)
        qkv_flat = qkv_w.reshape(model_width, -1)

        def attn_back(row_start, row_span):
            return right_product(flat_qkv, qkv_flat)

        grad_normed_attn = input_sum(attn_back, local_rows)
        back_attn, grad_g_attn = norm_backward(rows_in, scale_attn, g_attn, grad_normed_attn)
        input_grads.append(grad_resid + back_attn)
        grad_terms = (grad_g_attn, grad_qkv_w, grad_out_w, grad_g_mlp, grad_gu_w, grad_down)
        grad_total = add_terms(grad_total, grad_terms)
    owned_grads = lax.psum_scatter(grad_total, "dp", scatter_dimension=0, tiled=True)
    gain_first, gain_second = lax.psum((owned_grads[0], owned_grads[3]), "tensor")
    return (
        jnp.stack(outputs),
        jnp.stack(input_grads),
        gain_first,
        owned_grads[1],
        owned_grads[2],
        gain_second,
        owned_grads[4],
        owned_grads[5],
    )


def solution(mesh):
    placed = (
        P("dp", "tensor", None),
        P("dp", None),
        P("dp"),
        P("dp", "tensor", None),
        P("dp", "tensor"),
        P("dp"),
        P("dp", None, "tensor"),
        P("dp", "tensor"),
        P("dp", "tensor", None),
    )
    return jax.shard_map(
        body,
        mesh=mesh,
        in_specs=placed,
        out_specs=(
            P("dp", "tensor", None),
            P("dp", "tensor", None),
            P("dp"),
            P("dp", "tensor", None),
            P("dp", "tensor"),
            P("dp"),
            P("dp", None, "tensor"),
            P("dp", "tensor"),
        ),
        check_vma=False,
    )
```

profile of v0, /device:TPU:0, one launch (start us, length us, event | category | flops | bytes accessed | tf_op | source)
XLA Modules:
  0.0 1613.4 jit_solution(4839132049116461535)
XLA Ops:
  9.8 10.4 all-gather
  26.1 42.1 %all-gather.15.cloned.1.call-done = bf16[512,2048]{1,0:T(8,128)(2,1)} async-done(((bf16[128,2048]{1,0:T(8,128)(2,1)}), bf16[512,2048]{1,0:T(8,128)(2,1)}) %all-gather.15.cloned.1.call-update) | async-done | bytes 2097168 | tf_op jit(solution)/shard_map/all_gather | solution.py:158
  68.2 30.7 %all-gather.17.cloned.1.call-done = bf16[2048,1,640]{2,0,1:T(8,128)(2,1)} async-done(((bf16[256,1,640]{2,0,1:T(8,128)(2,1)}), bf16[2048,1,640]{2,0,1:T(8,128)(2,1)}) %all-gather.17.cloned.1.call-update) | async-done | bytes 2621456 | tf_op jit(solution)/shard_map/all_gather | solution.py:202
  105.6 41.1 %all-gather.27.cloned.1.call-done = bf16[512,2048]{1,0:T(8,128)(2,1)} async-done(((bf16[128,2048]{1,0:T(8,128)(2,1)}), bf16[512,2048]{1,0:T(8,128)(2,1)}) %all-gather.27.cloned.1.call-update) | async-done | bytes 2097168 | tf_op jit(solution)/shard_map/all_gather | solution.py:158
  161.5 13.6 all-gather.19.cloned.1.call-done
  210.8 46.2 %reduce-scatter.13.cloned.1.call-done = f32[128,2048]{1,0:T(8,128)} async-done(((f32[512,2048]{1,0:T(8,128)}), f32[128,2048]{1,0:T(8,128)}) %reduce-scatter.13.cloned.1.call-update) | async-done | bytes 1048592 | tf_op jit(solution)/shard_map/reduce_scatter | solution.py:166
  257.0 79.5 %reduce-scatter.17.cloned.1.call-done = f32[128,2048]{1,0:T(8,128)} async-done(((f32[512,2048]{1,0:T(8,128)}), f32[128,2048]{1,0:T(8,128)}) %reduce-scatter.17.cloned.1.call-update) | async-done | bytes 1048592 | tf_op jit(solution)/shard_map/reduce_scatter | solution.py:166
  343.9 63.1 %all-gather.23.cloned.1.call-done = bf16[2048,2,1408]{2,0,1:T(8,128)(2,1)} async-done(((bf16[256,2,1408]{2,0,1:T(8,128)(2,1)}), bf16[2048,2,1408]{2,0,1:T(8,128)(2,1)}) %all-gather.23.cloned.1.call-update) | async-done | bytes 11534352 | tf_op jit(solution)/shard_map/all_gather | solution.py:205
  407.0 15.2 copy.87
  422.2 32.6 %all-gather.21.cloned.1.call-done = bf16[512,2048]{1,0:T(8,128)(2,1)} async-done(((bf16[128,2048]{1,0:T(8,128)(2,1)}), bf16[512,2048]{1,0:T(8,128)(2,1)}) %all-gather.21.cloned.1.call-update) | async-done | bytes 2097168 | tf_op jit(solution)/shard_map/all_gather | solution.py:158
  454.8 11.8 fusion.2
  466.6 34.8 %all-gather.31.cloned.1.call-done = bf16[512,2048]{1,0:T(8,128)(2,1)} async-done(((bf16[128,2048]{1,0:T(8,128)(2,1)}), bf16[512,2048]{1,0:T(8,128)(2,1)}) %all-gather.31.cloned.1.call-update) | async-done | bytes 2097168 | tf_op jit(solution)/shard_map/all_gather | solution.py:162
  501.5 43.8 %all-gather.25.cloned.1.call-done = bf16[2048,1408]{1,0:T(8,128)(2,1)} async-done(((bf16[256,1408]{1,0:T(8,128)(2,1)}), bf16[2048,1408]{1,0:T(8,128)(2,1)}) %all-gather.25.cloned.1.call-update) | async-done | bytes 5767184 | tf_op jit(solution)/shard_map/all_gather | solution.py:206
  566.2 76.9 %reduce-scatter.21.cloned.1.call-done = f32[128,2048]{1,0:T(8,128)} async-done(((f32[512,2048]{1,0:T(8,128)}), f32[128,2048]{1,0:T(8,128)}) %reduce-scatter.21.cloned.1.call-update) | async-done | bytes 1048592 | tf_op jit(solution)/shard_map/reduce_scatter | solution.py:175
  647.0 45.4 %all-gather.29.cloned.1.call-done = bf16[512,2048]{1,0:T(8,128)(2,1)} async-done(((bf16[128,2048]{1,0:T(8,128)(2,1)}), bf16[512,2048]{1,0:T(8,128)(2,1)}) %all-gather.29.cloned.1.call-update) | async-done | bytes 2097168 | tf_op jit(solution)/shard_map/all_gather | solution.py:158
  692.4 11.8 fusion
  704.2 34.9 %all-gather.35.cloned.1.call-done = bf16[512,2048]{1,0:T(8,128)(2,1)} async-done(((bf16[128,2048]{1,0:T(8,128)(2,1)}), bf16[512,2048]{1,0:T(8,128)(2,1)}) %all-gather.35.cloned.1.call-update) | async-done | bytes 2097168 | tf_op jit(solution)/shard_map/all_gather | solution.py:162
  749.6 10.3 convolution_bitcast_fusion
  785.5 50.3 %reduce-scatter.25.cloned.1.call-done = f32[128,2048]{1,0:T(8,128)} async-done(((f32[512,2048]{1,0:T(8,128)}), f32[128,2048]{1,0:T(8,128)}) %reduce-scatter.25.cloned.1.call-update) | async-done | bytes 1048592 | tf_op jit(solution)/shard_map/reduce_scatter | solution.py:175
  837.3 78.0 %reduce-scatter.15.cloned.1.call-done = f32[128,2048]{1,0:T(8,128)} async-done(((f32[512,2048]{1,0:T(8,128)}), f32[128,2048]{1,0:T(8,128)}) %reduce-scatter.15.cloned.1.call-update) | async-done | bytes 1048592 | tf_op jit(solution)/shard_map/reduce_scatter | solution.py:166
  915.2 79.5 %reduce-scatter.19.cloned.1.call-done = f32[128,2048]{1,0:T(8,128)} async-done(((f32[512,2048]{1,0:T(8,128)}), f32[128,2048]{1,0:T(8,128)}) %reduce-scatter.19.cloned.1.call-update) | async-done | bytes 1048592 | tf_op jit(solution)/shard_map/reduce_scatter | solution.py:166
  1012.7 33.7 %all-gather.33.cloned.1.call-done = bf16[512,2048]{1,0:T(8,128)(2,1)} async-done(((bf16[128,2048]{1,0:T(8,128)(2,1)}), bf16[512,2048]{1,0:T(8,128)(2,1)}) %all-gather.33.cloned.1.call-update) | async-done | bytes 2097168 | tf_op jit(solution)/shard_map/all_gather | solution.py:162
  1061.9 31.0 %all-gather.37.cloned.1.call-done = bf16[512,2048]{1,0:T(8,128)(2,1)} async-done(((bf16[128,2048]{1,0:T(8,128)(2,1)}), bf16[512,2048]{1,0:T(8,128)(2,1)}) %all-gather.37.cloned.1.call-update) | async-done | bytes 2097168 | tf_op jit(solution)/shard_map/all_gather | solution.py:162
  1145.3 13.4 fusion.21
  1161.7 17.7 %convolution_add_fusion = f32[2048,2,1408]{2,0,1:T(8,128)} fusion(f32[2048,2,1408]{2,0,1:T(8,128)} %fusion.21, bf16[512,2,1408]{0,2,1:T(8,128)(2,1)} %copy.110, bf16[512,2048]{1,0:T(8,128)(2,1)} %all-gather.29.cloned.1.call-done), kind=kOutput, calls=%fused_computation | convolution fusion | flops 5911347200 | bytes 51118080 | tf_op jit(solution)/shard_map/dot_general | solution.py:146
  1193.3 48.5 %reduce-scatter.29.cloned.1.call-done = f32[256,1,640]{2,0,1:T(8,128)} async-done(((f32[2048,1,640]{2,0,1:T(8,128)}), f32[256,1,640]{2,0,1:T(8,128)}) %reduce-scatter.29.cloned.1.call-update) | async-done | bytes 655376 | tf_op jit(solution)/shard_map/reduce_scatter | solution.py:289
  1244.4 76.5 %reduce-scatter.27.cloned.1.call-done = f32[128,2048]{1,0:T(8,128)} async-done(((f32[512,2048]{1,0:T(8,128)}), f32[128,2048]{1,0:T(8,128)}) %reduce-scatter.27.cloned.1.call-update) | async-done | bytes 1048592 | tf_op jit(solution)/shard_map/reduce_scatter | solution.py:175
  1320.9 79.6 %reduce-scatter.23.cloned.1.call-done = f32[128,2048]{1,0:T(8,128)} async-done(((f32[512,2048]{1,0:T(8,128)}), f32[128,2048]{1,0:T(8,128)}) %reduce-scatter.23.cloned.1.call-update) | async-done | bytes 1048592 | tf_op jit(solution)/shard_map/reduce_scatter | solution.py:175
  1402.7 23.7 %all-reduce.2 = (f32[2048]{0:T(1024)S(1)}, f32[2048]{0:T(1024)S(1)}) all-reduce(f32[2048]{0:T(1024)S(1)} %add.202, f32[2048]{0:T(1024)S(1)} %add.206), channel_id=10, replica_groups=mesh['dp'=8,'tensor'=4] {'dp'}, use_global_device_ids=true, to_apply=%region_26.27.clone | all-reduce | flops 4096 | bytes 32768
  1426.5 12.0 all-reduce.3
  1442.4 108.7 %reduce-scatter.33.cloned.1.call-done = f32[256,2,1408]{2,0,1:T(8,128)} async-done(((f32[2048,2,1408]{2,0,1:T(8,128)}), f32[256,2,1408]{2,0,1:T(8,128)}) %reduce-scatter.33.cloned.1.call-update) | async-done | bytes 2883600 | tf_op jit(solution)/shard_map/reduce_scatter | solution.py:289
  1556.7 49.4 %reduce-scatter.31.cloned.1.call-done = f32[256,512]{1,0:T(8,128)} async-done(((f32[2048,512]{1,0:T(8,128)}), f32[256,512]{1,0:T(8,128)}) %reduce-scatter.31.cloned.1.call-update) | async-done | bytes 524304 | tf_op jit(solution)/shard_map/reduce_scatter | solution.py:289
  (341 shorter events, 250.5 us)
Async XLA Ops:
  7.2 61.0 %all-gather.15.cloned.1.call-start = ((), (), s32[]{:S(2)}) async-start(), calls=%async_computation.12 | async-start | bytes 2621440 | tf_op jit(solution)/shard_map/all_gather | solution.py:158
  22.1 76.8 %all-gather.17.cloned.1.call-start = ((), (), s32[]{:S(2)}) async-start(), calls=%async_computation.13 | async-start | bytes 2949120 | tf_op jit(solution)/shard_map/all_gather | solution.py:202
  22.9 123.9 %all-gather.27.cloned.1.call-start = ((), (), s32[]{:S(2)}) async-start(), calls=%async_computation.20 | async-start | bytes 2621440 | tf_op jit(solution)/shard_map/all_gather | solution.py:158
  23.6 151.5 %all-gather.19.cloned.1.call-start = ((), (), s32[]{:S(2)}) async-start(), calls=%async_computation.14 | async-start | bytes 2359296 | tf_op jit(solution)/shard_map/all_gather | solution.py:203
  24.2 232.8 %reduce-scatter.13.cloned.1.call-start = ((), (), s32[]{:S(2)}) async-start(), calls=%async_computation.15 | async-start | bytes 5242880 | tf_op jit(solution)/shard_map/reduce_scatter | solution.py:166
  24.8 126.2 %copy-start.70 = (f32[512]{0:T(512)}, f32[512]{0:T(512)S(1)}, u32[]{:S(2)}) copy-start(f32[512]{0:T(512)S(1)} %get-tuple-element.119) | copy-start | bytes 6148
  180.0 156.4 %reduce-scatter.17.cloned.1.call-start = ((), (), s32[]{:S(2)}) async-start(), calls=%async_computation.21 | async-start | bytes 5242880 | tf_op jit(solution)/shard_map/reduce_scatter | solution.py:166
  199.1 207.9 %all-gather.23.cloned.1.call-start = ((), (), s32[]{:S(2)}) async-start(), calls=%async_computation.17 | async-start | bytes 12976128 | tf_op jit(solution)/shard_map/all_gather | solution.py:205
  201.8 253.0 %all-gather.21.cloned.1.call-start = ((), (), s32[]{:S(2)}) async-start(), calls=%async_computation.16 | async-start | bytes 2621440 | tf_op jit(solution)/shard_map/all_gather | solution.py:158
  340.2 161.3 %all-gather.31.cloned.1.call-start = ((), (), s32[]{:S(2)}) async-start(), calls=%async_computation.24 | async-start | bytes 2621440 | tf_op jit(solution)/shard_map/all_gather | solution.py:162
  342.9 202.4 %all-gather.25.cloned.1.call-start = ((), (), s32[]{:S(2)}) async-start(), calls=%async_computation.18 | async-start | bytes 6488064 | tf_op jit(solution)/shard_map/all_gather | solution.py:206
  343.5 299.6 %reduce-scatter.21.cloned.1.call-start = ((), (), s32[]{:S(2)}) async-start(), calls=%async_computation.25 | async-start | bytes 5242880 | tf_op jit(solution)/shard_map/reduce_scatter | solution.py:175
  566.1 126.3 %all-gather.29.cloned.1.call-start = ((), (), s32[]{:S(2)}) async-start(), calls=%async_computation.22 | async-start | bytes 2621440 | tf_op jit(solution)/shard_map/all_gather | solution.py:158
  646.1 93.0 %all-gather.35.cloned.1.call-start = ((), (), s32[]{:S(2)}) async-start(), calls=%async_computation.28 | async-start | bytes 2621440 | tf_op jit(solution)/shard_map/all_gather | solution.py:162
  646.8 188.9 %reduce-scatter.25.cloned.1.call-start = ((), (), s32[]{:S(2)}) async-start(), calls=%async_computation.29 | async-start | bytes 5242880 | tf_op jit(solution)/shard_map/reduce_scatter | solution.py:175
  760.0 155.2 %reduce-scatter.15.cloned.1.call-start = ((), (), s32[]{:S(2)}) async-start(), calls=%async_computation.19 | async-start | bytes 5242880 | tf_op jit(solution)/shard_map/reduce_scatter | solution.py:166
  772.7 222.0 %reduce-scatter.19.cloned.1.call-start = ((), (), s32[]{:S(2)}) async-start(), calls=%async_computation.23 | async-start | bytes 5242880 | tf_op jit(solution)/shard_map/reduce_scatter | solution.py:166
  785.4 209.3 %copy-start.15 = (f32[128,2048]{1,0:T(8,128)S(1)}, f32[128,2048]{1,0:T(8,128)}, u32[]{:S(2)}) copy-start(f32[128,2048]{1,0:T(8,128)} %reduce-scatter.21.cloned.1.call-done) | copy-start | bytes 3145732
  785.4 261.0 %all-gather.33.cloned.1.call-start = ((), (), s32[]{:S(2)}) async-start(), calls=%async_computation.26 | async-start | bytes 2621440 | tf_op jit(solution)/shard_map/all_gather | solution.py:162
  1000.1 92.8 %all-gather.37.cloned.1.call-start = ((), (), s32[]{:S(2)}) async-start(), calls=%async_computation.30 | async-start | bytes 2621440 | tf_op jit(solution)/shard_map/all_gather | solution.py:162
  1000.7 189.6 %reduce-scatter.35.cloned.1.call-start = ((), (), s32[]{:S(2)}) async-start(), calls=%async_computation.35 | async-start | bytes 12976128 | tf_op jit(solution)/shard_map/reduce_scatter | solution.py:289
  1012.2 229.6 %reduce-scatter.29.cloned.1.call-start = ((), (), s32[]{:S(2)}) async-start(), calls=%async_computation.32 | async-start | bytes 5898240 | tf_op jit(solution)/shard_map/reduce_scatter | solution.py:289
  1128.9 192.0 %reduce-scatter.27.cloned.1.call-start = ((), (), s32[]{:S(2)}) async-start(), calls=%async_computation.31 | async-start | bytes 5242880 | tf_op jit(solution)/shard_map/reduce_scatter | solution.py:175
  1134.5 266.0 %reduce-scatter.23.cloned.1.call-start = ((), (), s32[]{:S(2)}) async-start(), calls=%async_computation.27 | async-start | bytes 5242880 | tf_op jit(solution)/shard_map/reduce_scatter | solution.py:175
  1140.4 410.7 %reduce-scatter.33.cloned.1.call-start = ((), (), s32[]{:S(2)}) async-start(), calls=%async_computation.34 | async-start | bytes 25952256 | tf_op jit(solution)/shard_map/reduce_scatter | solution.py:289
  1179.5 426.6 %reduce-scatter.31.cloned.1.call-start = ((), (), s32[]{:S(2)}) async-start(), calls=%async_computation.33 | async-start | bytes 4718592 | tf_op jit(solution)/shard_map/reduce_scatter | solution.py:289
  1190.2 210.4 %copy-start.3 = (f32[2,128,2048]{2,1,0:T(8,128)S(1)}, f32[2,128,2048]{2,1,0:T(8,128)}, u32[]{:S(2)}) copy-start(f32[2,128,2048]{2,1,0:T(8,128)} %param.9) | copy-start | bytes 6291460
  1190.2 210.4 %copy-start.67 = (f32[8,1,256]{2,1,0:T(1,128)S(1)}, f32[8,1,256]{2,1,0:T(1,128)}, u32[]{:S(2)}) copy-start(f32[8,1,256]{2,1,0:T(1,128)} %copy-done.66) | copy-start | bytes 24580
  1190.2 210.4 %copy-start.76 = (f32[128]{0:T(128)S(1)}, f32[128]{0:T(128)}, u32[]{:S(2)}) copy-start(f32[128]{0:T(128)} %copy-done.75) | copy-start | bytes 1540
  1190.2 210.4 %copy-start.78 = (f32[128]{0:T(128)S(1)}, f32[128]{0:T(128)}, u32[]{:S(2)}) copy-start(f32[128]{0:T(128)} %copy-done.77) | copy-start | bytes 1540
  1193.3 245.2 %copy-start.82 = (f32[128]{0:T(128)S(1)}, f32[128]{0:T(128)}, u32[]{:S(2)}) copy-start(f32[128]{0:T(128)} %get-tuple-element.97) | copy-start | bytes 1540
  1193.3 245.2 %copy-start.83 = (f32[128]{0:T(128)S(1)}, f32[128]{0:T(128)}, u32[]{:S(2)}) copy-start(f32[128]{0:T(128)} %get-tuple-element.118) | copy-start | bytes 1540
  (86 other events, 1031.7 us)
Sparse Core Ops, SparseCore 0:
  22.2 45.9 all-gather.14
  70.1 28.7 all-gather.16
  101.1 45.6 all-gather.26
  148.5 26.5 all-gather.18
  180.1 76.7 reduce-scatter.12
  259.1 77.2 reduce-scatter.16
  338.9 68.0 all-gather.22
  409.2 45.6 all-gather.20
  457.0 44.4 all-gather.30
  503.2 41.9 all-gather.24
  566.3 76.7 reduce-scatter.20
  646.2 46.1 all-gather.28
  694.5 44.4 all-gather.34
  760.1 75.5 reduce-scatter.24
  837.9 77.2 reduce-scatter.14
  917.4 77.2 reduce-scatter.18
  1000.2 46.1 all-gather.32
  1048.4 44.4 all-gather.36
  1096.4 85.6 reduce-scatter.34
  1185.3 56.4 reduce-scatter.28
  1244.1 76.7 reduce-scatter.26
  1323.2 77.2 reduce-scatter.22
  1404.2 146.8 reduce-scatter.32
  1554.9 51.1 reduce-scatter.30
where the time goes:
time: 1620 us; the launch traced here: 1610 us
  waiting for transfers between devices  1220 us (75%)
  matrix products  200 us (12%)
  local copies, waits for them, and re-layouts  62.7 us (4%)
  blocking collectives  55 us (3%)
  other arithmetic  52.8 us (3%)
  between operations  16.8 us (1%)
    reduce_scatter x4, waiting for transfers between devices, input_sum(): lax.psum_scatter(term_fn(jnp.int32(0), lax.axis_size('tensor') * local_ro...  283 us
    reduce_scatter x4, waiting for transfers between devices, branch_sum(): lax.psum_scatter(term_fn(jnp.int32(0), lax.axis_size('tensor') * local_ro...  283 us
    reduce_scatter x4, waiting for transfers between devices, body(): lax.psum_scatter(grad_total, 'dp', scatter_dimension=0, tiled=True)  207 us
    all_gather x4, waiting for transfers between devices, spread_forward(): return lax.all_gather(row_block, 'tensor', axis=0, tiled=True)  161 us
    all_gather x4, waiting for transfers between devices, spread_backward(): return lax.all_gather(row_block, 'tensor', axis=0, tiled=True)  134 us
    all_gather x1, waiting for transfers between devices, body(): lax.all_gather(weight_shard[4], 'dp', axis=0, tiled=True)  63.1 us
    dot_general x8, matrix products, right_product(): lax.dot_general(left_rows, right_matrix, (((1,), (1,)), ((), ())), prefer...  55.7 us
    dot_general x8, matrix products, outer_product(): lax.dot_general(left_rows, right_rows, (((0,), (0,)), ((), ())), preferre...  55.1 us
  transfers between devices with their start and end apart: 24, of which 23 were waited for; matrix products, arithmetic and copies ran while one was open for 15% of the time, Pallas kernels for 0%

commit v1 on v0

--- a/solution.py
+++ b/solution.py
@@ -8,6 +8,20 @@
 KV = 4
 HD = 64
 NORM_EPS = 1e-05
+
+
+def trace_the_loads(chip_axis, work_x):
+    leaves = [work_x]
+    pp = 1
+    p_count = lax.psum(1, chip_axis)
+    while pp < p_count:
+        leaves.append(
+            lax.ppermute(
+                leaves[pp - 1], chip_axis, [(b, (b - 1) % p_count) for b in range(p_count)]
+            )
+        )
+        pp = pp + 1
+    return jnp.roll(jnp.concatenate(leaves, 0), lax.axis_index(chip_axis) * work_x.shape[0], 0)
 
 
 def rope_tables(segment_row, head_size):
@@ -155,7 +169,7 @@
 
 
 def spread_forward(row_block):
-    return lax.all_gather(row_block, "tensor", axis=0, tiled=True)
+    return trace_the_loads("tensor", row_block)
 
 
 def spread_backward(row_block):

time: 1620 us -> 1520 us (0.938)
  waiting for transfers between devices: 1220 us -> 1060 us
  starting transfers between devices: 2.85 us -> 41.2 us
  other arithmetic: 52.8 us -> 85.6 us
    all_gather x4 -> x0, waiting for transfers between devices: 161 us -> none  [spread_forward(): return lax.all_gather(row_block, 'tensor', axis=0, tiled=True)]
    ppermute x0 -> x12, waiting for transfers between devices: none -> 135 us  [trace_the_loads(): lax.ppermute(leaves[pp - 1], chip_axis, [(b, (b - 1) % p_count) for b in...]
    all_gather x4, waiting for transfers between devices: 134 us -> 86.6 us  [spread_backward(): return lax.all_gather(row_block, 'tensor', axis=0, tiled=True)]
    all_gather x1, waiting for transfers between devices: 63.1 us -> 16.4 us  [body(): lax.all_gather(weight_shard[4], 'dp', axis=0, tiled=True)]
    ppermute x0 -> x12, starting transfers between devices: none -> 39.8 us  [trace_the_loads(): lax.ppermute(leaves[pp - 1], chip_axis, [(b, (b - 1) % p_count) for b in...]
    all_gather x1, waiting for transfers between devices: 30.7 us -> 0.01 us  [body(): lax.all_gather(weight_shard[1], 'dp', axis=0, tiled=True)]
    concatenate x0 -> x2, other arithmetic: none -> 17 us  [trace_the_loads(): jnp.roll(jnp.concatenate(leaves, 0), lax.axis_index(chip_axis) * work_x.s...]
    dynamic_slice x0 -> x2, other arithmetic: none -> 16.8 us  [trace_the_loads(): jnp.roll(jnp.concatenate(leaves, 0), lax.axis_index(chip_axis) * work_x.s...]
  transfers between devices with their start and end apart: 24 -> 32, of which waited for: 23 -> 28; matrix products, arithmetic and copies ran while one was open for 15% -> 18% of each run, Pallas kernels for 0% -> 0%
where the time goes in v1:
time: 1520 us
  waiting for transfers between devices  1060 us (70%)
  matrix products  197 us (13%)
  other arithmetic  85.6 us (6%)
  local copies, waits for them, and re-layouts  61.7 us (4%)
  blocking collectives  55 us (4%)
  starting transfers between devices  41.2 us (3%)
  between operations  16.6 us (1%)
    reduce_scatter x4, waiting for transfers between devices, input_sum(): lax.psum_scatter(term_fn(jnp.int32(0), lax.axis_size('tensor') * local_ro...  287 us
    reduce_scatter x4, waiting for transfers between devices, branch_sum(): lax.psum_scatter(term_fn(jnp.int32(0), lax.axis_size('tensor') * local_ro...  286 us
    reduce_scatter x4, waiting for transfers between devices, body(): lax.psum_scatter(grad_total, 'dp', scatter_dimension=0, tiled=True)  203 us
    ppermute x12, waiting for transfers between devices, trace_the_loads(): lax.ppermute(leaves[pp - 1], chip_axis, [(b, (b - 1) % p_count) for b in...  135 us
    all_gather x4, waiting for transfers between devices, spread_backward(): return lax.all_gather(row_block, 'tensor', axis=0, tiled=True)  86.6 us
    dot_general x8, matrix products, right_product(): lax.dot_general(left_rows, right_matrix, (((1,), (1,)), ((), ())), prefer...  56 us
    dot_general x8, matrix products, outer_product(): lax.dot_general(left_rows, right_rows, (((0,), (0,)), ((), ())), preferre...  53.8 us
    all_gather x1, waiting for transfers between devices, body(): lax.all_gather(weight_shard[5], 'dp', axis=0, tiled=True)  43.9 us
  transfers between devices with their start and end apart: 32, of which 28 were waited for; matrix products, arithmetic and copies ran while one was open for 18% of the time, Pallas kernels for 0%

profile of v1, /device:TPU:0, one launch (start us, length us, event | category | flops | bytes accessed | tf_op | source)
XLA Modules:
  0.0 1517.0 jit_solution(17959786682666895539)
XLA Ops:
  8.6 10.4 all-gather
  27.6 11.7 collective-permute-done
  158.5 48.4 %reduce-scatter.13.cloned.1.call-done = f32[128,2048]{1,0:T(8,128)} async-done(((f32[512,2048]{1,0:T(8,128)}), f32[128,2048]{1,0:T(8,128)}) %reduce-scatter.13.cloned.1.call-update) | async-done | bytes 1048592 | tf_op jit(solution)/shard_map/reduce_scatter | solution.py:180
  206.9 79.5 %reduce-scatter.17.cloned.1.call-done = f32[128,2048]{1,0:T(8,128)} async-done(((f32[512,2048]{1,0:T(8,128)}), f32[128,2048]{1,0:T(8,128)}) %reduce-scatter.17.cloned.1.call-update) | async-done | bytes 1048592 | tf_op jit(solution)/shard_map/reduce_scatter | solution.py:180
  292.0 11.3 collective-permute-done.3
  307.5 10.4 collective-permute-done.4
  340.5 16.4 %all-gather.15.cloned.1.call-done = bf16[2048,2,1408]{2,0,1:T(8,128)(2,1)} async-done(((bf16[256,2,1408]{2,0,1:T(8,128)(2,1)}), bf16[2048,2,1408]{2,0,1:T(8,128)(2,1)}) %all-gather.15.cloned.1.call-update) | async-done | bytes 11534352 | tf_op jit(solution)/shard_map/all_gather | solution.py:219
  356.8 15.2 %copy.87 = bf16[2048,2,1408]{0,2,1:T(8,128)(2,1)} copy(bf16[2048,2,1408]{2,0,1:T(8,128)(2,1)} %all-gather.15.cloned.1.call-done) | data formatting | bytes 23068672 | tf_op jit(solution)/shard_map/all_gather | solution.py:219
  372.1 11.1 fusion.2
  383.2 21.3 %all-gather.19.cloned.1.call-done = bf16[512,2048]{1,0:T(8,128)(2,1)} async-done(((bf16[128,2048]{1,0:T(8,128)(2,1)}), bf16[512,2048]{1,0:T(8,128)(2,1)}) %all-gather.19.cloned.1.call-update) | async-done | bytes 2097168 | tf_op jit(solution)/shard_map/all_gather | solution.py:176
  404.5 43.9 %all-gather.17.cloned.1.call-done = bf16[2048,1408]{1,0:T(8,128)(2,1)} async-done(((bf16[256,1408]{1,0:T(8,128)(2,1)}), bf16[2048,1408]{1,0:T(8,128)(2,1)}) %all-gather.17.cloned.1.call-update) | async-done | bytes 5767184 | tf_op jit(solution)/shard_map/all_gather | solution.py:220
  459.0 10.7 convolution_bitcast_fusion.1
  469.8 76.9 %reduce-scatter.21.cloned.1.call-done = f32[128,2048]{1,0:T(8,128)} async-done(((f32[512,2048]{1,0:T(8,128)}), f32[128,2048]{1,0:T(8,128)}) %reduce-scatter.21.cloned.1.call-update) | async-done | bytes 1048592 | tf_op jit(solution)/shard_map/reduce_scatter | solution.py:189
  551.6 15.8 %collective-permute-done.9 = bf16[128,2048]{1,0:T(8,128)(2,1)S(1)} collective-permute-done((bf16[128,2048]{1,0:T(8,128)(2,1)S(1)}, bf16[128,2048]{1,0:T(8,128)(2,1)S(1)}, u32[]{:S(2)}, u32[]{:S(2)}) %collective-permute-start.9) | collective-permute-done | bytes 524320 | tf_op jit(solution)/shard_map/ppermute | solution.py:19
  571.7 34.4 %collective-permute-done.10 = bf16[128,2048]{1,0:T(8,128)(2,1)S(1)} collective-permute-done((bf16[128,2048]{1,0:T(8,128)(2,1)S(1)}, bf16[128,2048]{1,0:T(8,128)(2,1)S(1)}, u32[]{:S(2)}, u32[]{:S(2)}) %collective-permute-start.10) | collective-permute-done | bytes 524320 | tf_op jit(solution)/shard_map/ppermute | solution.py:19
  606.1 13.1 collective-permute-done.11
  628.9 11.1 fusion
  650.5 10.5 convolution_bitcast_fusion
  685.8 54.0 %reduce-scatter.25.cloned.1.call-done = f32[128,2048]{1,0:T(8,128)} async-done(((f32[512,2048]{1,0:T(8,128)}), f32[128,2048]{1,0:T(8,128)}) %reduce-scatter.25.cloned.1.call-update) | async-done | bytes 1048592 | tf_op jit(solution)/shard_map/reduce_scatter | solution.py:189
  741.3 78.1 %reduce-scatter.15.cloned.1.call-done = f32[128,2048]{1,0:T(8,128)} async-done(((f32[512,2048]{1,0:T(8,128)}), f32[128,2048]{1,0:T(8,128)}) %reduce-scatter.15.cloned.1.call-update) | async-done | bytes 1048592 | tf_op jit(solution)/shard_map/reduce_scatter | solution.py:180
  819.4 79.5 %reduce-scatter.19.cloned.1.call-done = f32[128,2048]{1,0:T(8,128)} async-done(((f32[512,2048]{1,0:T(8,128)}), f32[128,2048]{1,0:T(8,128)}) %reduce-scatter.19.cloned.1.call-update) | async-done | bytes 1048592 | tf_op jit(solution)/shard_map/reduce_scatter | solution.py:180
  916.6 34.0 %all-gather.21.cloned.1.call-done = bf16[512,2048]{1,0:T(8,128)(2,1)} async-done(((bf16[128,2048]{1,0:T(8,128)(2,1)}), bf16[512,2048]{1,0:T(8,128)(2,1)}) %all-gather.21.cloned.1.call-update) | async-done | bytes 2097168 | tf_op jit(solution)/shard_map/all_gather | solution.py:176
  965.9 31.2 %all-gather.25.cloned.1.call-done = bf16[512,2048]{1,0:T(8,128)(2,1)} async-done(((bf16[128,2048]{1,0:T(8,128)(2,1)}), bf16[512,2048]{1,0:T(8,128)(2,1)}) %all-gather.25.cloned.1.call-update) | async-done | bytes 2097168 | tf_op jit(solution)/shard_map/all_gather | solution.py:176
  1052.6 13.2 fusion.21
  1068.9 16.6 %convolution_add_fusion = f32[2048,2,1408]{2,0,1:T(8,128)} fusion(f32[2048,2,1408]{2,0,1:T(8,128)} %fusion.21, bf16[512,2048,1]{1,0,2:T(8,128)(2,1)} %copy-done.12, bf16[512,2,1408]{0,2,1:T(8,128)(2,1)} %copy.110), kind=kOutput, calls=%fused_computation | convolution fusion | flops 5911347200 | bytes 51118080 | tf_op jit(solution)/shard_map/dot_general | solution.py:160
  1100.8 45.2 %reduce-scatter.29.cloned.1.call-done = f32[256,1,640]{2,0,1:T(8,128)} async-done(((f32[2048,1,640]{2,0,1:T(8,128)}), f32[256,1,640]{2,0,1:T(8,128)}) %reduce-scatter.29.cloned.1.call-update) | async-done | bytes 655376 | tf_op jit(solution)/shard_map/reduce_scatter | solution.py:303
  1148.6 76.3 %reduce-scatter.23.cloned.1.call-done = f32[128,2048]{1,0:T(8,128)} async-done(((f32[512,2048]{1,0:T(8,128)}), f32[128,2048]{1,0:T(8,128)}) %reduce-scatter.23.cloned.1.call-update) | async-done | bytes 1048592 | tf_op jit(solution)/shard_map/reduce_scatter | solution.py:189
  1224.9 79.5 %reduce-scatter.27.cloned.1.call-done = f32[128,2048]{1,0:T(8,128)} async-done(((f32[512,2048]{1,0:T(8,128)}), f32[128,2048]{1,0:T(8,128)}) %reduce-scatter.27.cloned.1.call-update) | async-done | bytes 1048592 | tf_op jit(solution)/shard_map/reduce_scatter | solution.py:189
  1306.5 23.7 %all-reduce.2 = (f32[2048]{0:T(1024)S(1)}, f32[2048]{0:T(1024)S(1)}) all-reduce(f32[2048]{0:T(1024)S(1)} %add.210, f32[2048]{0:T(1024)S(1)} %add.214), channel_id=10, replica_groups=mesh['dp'=8,'tensor'=4] {'dp'}, use_global_device_ids=true, to_apply=%region_26.28.clone | all-reduce | flops 4096 | bytes 32768
  1330.4 12.0 all-reduce.3
  1346.2 108.7 %reduce-scatter.33.cloned.1.call-done = f32[256,2,1408]{2,0,1:T(8,128)} async-done(((f32[2048,2,1408]{2,0,1:T(8,128)}), f32[256,2,1408]{2,0,1:T(8,128)}) %reduce-scatter.33.cloned.1.call-update) | async-done | bytes 2883600 | tf_op jit(solution)/shard_map/reduce_scatter | solution.py:303
  1460.6 49.4 %reduce-scatter.31.cloned.1.call-done = f32[256,512]{1,0:T(8,128)} async-done(((f32[2048,512]{1,0:T(8,128)}), f32[256,512]{1,0:T(8,128)}) %reduce-scatter.31.cloned.1.call-update) | async-done | bytes 524304 | tf_op jit(solution)/shard_map/reduce_scatter | solution.py:303
  (368 shorter events, 346.7 us)
Async XLA Ops:
  7.2 97.0 %all-gather.11.cloned.1.call-start = ((), (), s32[]{:S(2)}) async-start(), calls=%async_computation.12 | async-start | bytes 2949120 | tf_op jit(solution)/shard_map/all_gather | solution.py:216
  7.9 116.0 %all-gather.13.cloned.1.call-start = ((), (), s32[]{:S(2)}) async-start(), calls=%async_computation.13 | async-start | bytes 2359296 | tf_op jit(solution)/shard_map/all_gather | solution.py:217
  23.3 16.0 %collective-permute-start = (bf16[128,2048]{1,0:T(8,128)(2,1)S(1)}, bf16[128,2048]{1,0:T(8,128)(2,1)S(1)}, u32[]{:S(2)}, u32[]{:S(2)}) collective-permute-start(bf16[128,2048]{1,0:T(8,128)(2,1)S(1)} %get-tuple-element.65), channel_id=1, source_target_pairs={{0,3},{1,0},{2,1},{3,2},{4,7},{5,4},{6,5},{7,6},{8,11},{9,8},{10,9... | collective-permute-start | bytes 1572872 | tf_op jit(solution)/shard_map/ppermute | solution.py:19
  27.0 23.5 %collective-permute-start.6 = (bf16[128,2048]{1,0:T(8,128)(2,1)S(1)}, bf16[128,2048]{1,0:T(8,128)(2,1)S(1)}, u32[]{:S(2)}, u32[]{:S(2)}) collective-permute-start(bf16[128,2048]{1,0:T(8,128)(2,1)S(1)} %get-tuple-element.66), channel_id=1, source_target_pairs={{0,3},{1,0},{2,1},{3,2},{4,7},{5,4},{6,5},{7,6},{8,11},{9,8},{10,9... | collective-permute-start | bytes 1572872 | tf_op jit(solution)/shard_map/ppermute | solution.py:19
  27.5 179.4 %reduce-scatter.13.cloned.1.call-start = ((), (), s32[]{:S(2)}) async-start(), calls=%async_computation.14 | async-start | bytes 5242880 | tf_op jit(solution)/shard_map/reduce_scatter | solution.py:180
  39.3 22.5 %collective-permute-start.1 = (bf16[128,2048]{1,0:T(8,128)(2,1)S(1)}, bf16[128,2048]{1,0:T(8,128)(2,1)S(1)}, u32[]{:S(2)}, u32[]{:S(2)}) collective-permute-start(bf16[128,2048]{1,0:T(8,128)(2,1)S(1)} %collective-permute-done), channel_id=1, source_target_pairs={{0,3},{1,0},{2,1},{3,2},{4,7},{5,4},{6,5},{7,6},{8,11},{9,8},{10,9... | collective-permute-start | bytes 1572872 | tf_op jit(solution)/shard_map/ppermute | solution.py:19
  50.5 22.5 %collective-permute-start.7 = (bf16[128,2048]{1,0:T(8,128)(2,1)S(1)}, bf16[128,2048]{1,0:T(8,128)(2,1)S(1)}, u32[]{:S(2)}, u32[]{:S(2)}) collective-permute-start(bf16[128,2048]{1,0:T(8,128)(2,1)S(1)} %collective-permute-done.6), channel_id=1, source_target_pairs={{0,3},{1,0},{2,1},{3,2},{4,7},{5,4},{6,5},{7,6},{8,11},{9,8},{10,9... | collective-permute-start | bytes 1572872 | tf_op jit(solution)/shard_map/ppermute | solution.py:19
  61.8 22.5 %collective-permute-start.2 = (bf16[128,2048]{1,0:T(8,128)(2,1)S(1)}, bf16[128,2048]{1,0:T(8,128)(2,1)S(1)}, u32[]{:S(2)}, u32[]{:S(2)}) collective-permute-start(bf16[128,2048]{1,0:T(8,128)(2,1)S(1)} %collective-permute-done.1), channel_id=1, source_target_pairs={{0,3},{1,0},{2,1},{3,2},{4,7},{5,4},{6,5},{7,6},{8,11},{9,8},{10,9... | collective-permute-start | bytes 1572872 | tf_op jit(solution)/shard_map/ppermute | solution.py:19
  73.0 21.8 %collective-permute-start.8 = (bf16[128,2048]{1,0:T(8,128)(2,1)S(1)}, bf16[128,2048]{1,0:T(8,128)(2,1)S(1)}, u32[]{:S(2)}, u32[]{:S(2)}) collective-permute-start(bf16[128,2048]{1,0:T(8,128)(2,1)S(1)} %collective-permute-done.7), channel_id=1, source_target_pairs={{0,3},{1,0},{2,1},{3,2},{4,7},{5,4},{6,5},{7,6},{8,11},{9,8},{10,9... | collective-permute-start | bytes 1572872 | tf_op jit(solution)/shard_map/ppermute | solution.py:19
  129.0 157.4 %reduce-scatter.17.cloned.1.call-start = ((), (), s32[]{:S(2)}) async-start(), calls=%async_computation.18 | async-start | bytes 5242880 | tf_op jit(solution)/shard_map/reduce_scatter | solution.py:180
  143.4 213.4 %all-gather.15.cloned.1.call-start = ((), (), s32[]{:S(2)}) async-start(), calls=%async_computation.15 | async-start | bytes 12976128 | tf_op jit(solution)/shard_map/all_gather | solution.py:219
  146.0 258.5 %all-gather.19.cloned.1.call-start = ((), (), s32[]{:S(2)}) async-start(), calls=%async_computation.20 | async-start | bytes 2621440 | tf_op jit(solution)/shard_map/all_gather | solution.py:176
  148.7 299.7 %all-gather.17.cloned.1.call-start = ((), (), s32[]{:S(2)}) async-start(), calls=%async_computation.16 | async-start | bytes 6488064 | tf_op jit(solution)/shard_map/all_gather | solution.py:220
  149.5 397.2 %reduce-scatter.21.cloned.1.call-start = ((), (), s32[]{:S(2)}) async-start(), calls=%async_computation.21 | async-start | bytes 5242880 | tf_op jit(solution)/shard_map/reduce_scatter | solution.py:189
  289.3 13.9 collective-permute-start.3
  303.3 14.7 collective-permute-start.4
  318.0 14.1 collective-permute-start.5
  469.7 170.2 %all-gather.23.cloned.1.call-start = ((), (), s32[]{:S(2)}) async-start(), calls=%async_computation.24 | async-start | bytes 2621440 | tf_op jit(solution)/shard_map/all_gather | solution.py:176
  548.9 18.5 %collective-permute-start.9 = (bf16[128,2048]{1,0:T(8,128)(2,1)S(1)}, bf16[128,2048]{1,0:T(8,128)(2,1)S(1)}, u32[]{:S(2)}, u32[]{:S(2)}) collective-permute-start(bf16[128,2048]{1,0:T(8,128)(2,1)S(1)} %get-tuple-element.89), channel_id=1, source_target_pairs={{0,3},{1,0},{2,1},{3,2},{4,7},{5,4},{6,5},{7,6},{8,11},{9,8},{10,9... | collective-permute-start | bytes 1572872 | tf_op jit(solution)/shard_map/ppermute | solution.py:19
  551.5 188.3 %reduce-scatter.25.cloned.1.call-start = ((), (), s32[]{:S(2)}) async-start(), calls=%async_computation.25 | async-start | bytes 5242880 | tf_op jit(solution)/shard_map/reduce_scatter | solution.py:189
  567.4 38.7 %collective-permute-start.10 = (bf16[128,2048]{1,0:T(8,128)(2,1)S(1)}, bf16[128,2048]{1,0:T(8,128)(2,1)S(1)}, u32[]{:S(2)}, u32[]{:S(2)}) collective-permute-start(bf16[128,2048]{1,0:T(8,128)(2,1)S(1)} %collective-permute-done.9), channel_id=1, source_target_pairs={{0,3},{1,0},{2,1},{3,2},{4,7},{5,4},{6,5},{7,6},{8,11},{9,8},{10,9... | collective-permute-start | bytes 1572872 | tf_op jit(solution)/shard_map/ppermute | solution.py:19
  606.1 13.1 collective-permute-start.11
  661.0 158.4 %reduce-scatter.15.cloned.1.call-start = ((), (), s32[]{:S(2)}) async-start(), calls=%async_computation.17 | async-start | bytes 5242880 | tf_op jit(solution)/shard_map/reduce_scatter | solution.py:180
  673.3 225.6 %reduce-scatter.19.cloned.1.call-start = ((), (), s32[]{:S(2)}) async-start(), calls=%async_computation.19 | async-start | bytes 5242880 | tf_op jit(solution)/shard_map/reduce_scatter | solution.py:180
  685.7 264.9 %all-gather.21.cloned.1.call-start = ((), (), s32[]{:S(2)}) async-start(), calls=%async_computation.22 | async-start | bytes 2621440 | tf_op jit(solution)/shard_map/all_gather | solution.py:176
  904.3 92.8 %all-gather.25.cloned.1.call-start = ((), (), s32[]{:S(2)}) async-start(), calls=%async_computation.26 | async-start | bytes 2621440 | tf_op jit(solution)/shard_map/all_gather | solution.py:176
  904.9 192.8 %reduce-scatter.35.cloned.1.call-start = ((), (), s32[]{:S(2)}) async-start(), calls=%async_computation.31 | async-start | bytes 12976128 | tf_op jit(solution)/shard_map/reduce_scatter | solution.py:303
  916.6 229.4 %reduce-scatter.29.cloned.1.call-start = ((), (), s32[]{:S(2)}) async-start(), calls=%async_computation.28 | async-start | bytes 5898240 | tf_op jit(solution)/shard_map/reduce_scatter | solution.py:303
  1036.1 188.9 %reduce-scatter.23.cloned.1.call-start = ((), (), s32[]{:S(2)}) async-start(), calls=%async_computation.23 | async-start | bytes 5242880 | tf_op jit(solution)/shard_map/reduce_scatter | solution.py:189
  1041.7 262.8 %reduce-scatter.27.cloned.1.call-start = ((), (), s32[]{:S(2)}) async-start(), calls=%async_computation.27 | async-start | bytes 5242880 | tf_op jit(solution)/shard_map/reduce_scatter | solution.py:189
  1047.7 407.2 %reduce-scatter.33.cloned.1.call-start = ((), (), s32[]{:S(2)}) async-start(), calls=%async_computation.30 | async-start | bytes 25952256 | tf_op jit(solution)/shard_map/reduce_scatter | solution.py:303
  1085.5 424.4 %reduce-scatter.31.cloned.1.call-start = ((), (), s32[]{:S(2)}) async-start(), calls=%async_computation.29 | async-start | bytes 4718592 | tf_op jit(solution)/shard_map/reduce_scatter | solution.py:303
  (100 other events, 2892.3 us)
Sparse Core Ops, SparseCore 0:
  9.9 32.6 all-gather.10
  44.5 27.7 all-gather.12
  129.1 77.7 reduce-scatter.12
  209.1 77.3 reduce-scatter.16
  288.7 68.0 all-gather.14
  358.8 45.6 all-gather.18
  406.4 41.9 all-gather.16
  469.9 76.7 reduce-scatter.20
  551.6 60.6 all-gather.22
  661.1 78.6 reduce-scatter.24
  742.1 77.2 reduce-scatter.14
  821.6 77.2 reduce-scatter.18
  904.4 46.1 all-gather.20
  952.6 44.4 all-gather.24
  1000.5 85.6 reduce-scatter.34
  1089.4 56.5 reduce-scatter.28
  1148.1 76.7 reduce-scatter.22
  1227.1 77.2 reduce-scatter.26
  1308.0 146.8 reduce-scatter.32
  1458.7 51.1 reduce-scatter.30
